TPU v7x, 32 devices: a whole 2x2x4 slice. The times are simulated.
32 devices in a mesh: freq: 8 (over z, x), tm: 4 (over y, core).
Axes of the slice: x: 2, y: 2, z: 4, core: 2. Of those that a mesh axis runs over, the one named last changes fastest.
Arguments:
- vis: bfloat16 [16, 8, 16, 2, 128, 128], P('freq', 'tm'), may hold values from -6 to 6
- model: bfloat16 [16, 8, 16, 2, 128, 128], P('freq', 'tm'), may hold values from -6 to 6
- block_rows: int32 [16, 8, 16], P('freq', 'tm'), may hold values from 0 to 15
- block_cols: int32 [16, 8, 16], P('freq', 'tm'), may hold values from 0 to 15
- flags: int32 [16, 8, 16], P('freq', 'tm'), may hold values 0 or 1
- prior: float32 [16, 8, 2, 2048], P('freq', 'tm'), may hold values from -6 to 6
- couplings: float32 [3, 2048], replicated, may hold values from 0.1 to 0.6
- damping: float32 [2048], replicated, may hold values from 8 to 128
Outputs:
- gains: float32 [16, 8, 2, 2048], P('freq', 'tm')
- changes: float32 [4], replicated
All inputs are finite; a program needn't handle non-finite values. No bound on the sum of `flags` on one device may be relied on, other than what follows from the above.
Results may differ from a plain program's by a relative error of at most 0.0003.
Values sent between devices are 32-bit elements; how exact they have to be, the bound alone decides.
A program may use at most 64 MiB of HBM per device.

v0:
```python
import jax
import jax.numpy as jnp
from jax import lax
from jax.sharding import PartitionSpec as P

ITERS = 4


def extended(block, sides, width, periodic):
    for axis, dim in sides:
        count = lax.axis_size(axis)
        forward = [(i, i + 1) for i in range(count - 1)]
        if periodic:
            forward.append((count - 1, 0))
        backward = [(target, source) for source, target in forward]
        low = lax.ppermute(
            lax.slice_in_dim(block, block.shape[dim] - width, None, axis=dim), axis, forward
        )
        high = lax.ppermute(lax.slice_in_dim(block, 0, width, axis=dim), axis, backward)
        block = jnp.concatenate([low, block, high], axis=dim)
    return block


def shifted(value, axis, steps):
    count = lax.axis_size(axis)
    pairs = [(source, (source + steps) % count) for source in range(count)]
    return lax.ppermute(value, axis, pairs)


def tile_terms(gains, rows, cols, flags, vis, model):
    width = vis.shape[-1]
    blocks = gains.shape[-1] // width
    count = gains.shape[0]
    gain_blocks = gains.reshape(count, 2, blocks, width)
    labels = jnp.arange(blocks, dtype=jnp.int32)
    row_hot = (rows[..., None] == labels).astype(jnp.float32)
    col_hot = (cols[..., None] == labels).astype(jnp.float32)
    row_gain = jnp.einsum("kbn,kcnr->kbcr", row_hot, gain_blocks, precision=lax.Precision.HIGHEST)
    grow_re = row_gain[:, :, 0][..., None]
    grow_im = row_gain[:, :, 1][..., None]
    model_re = model[:, :, 0].astype(jnp.float32)
    model_im = model[:, :, 1].astype(jnp.float32)
    vis_re = vis[:, :, 0].astype(jnp.float32)
    vis_im = vis[:, :, 1].astype(jnp.float32)
    zeta_re = grow_re * model_re - grow_im * model_im
    zeta_im = grow_re * model_im + grow_im * model_re
    num_re = jnp.sum(vis_re * zeta_re + vis_im * zeta_im, axis=-2)
    num_im = jnp.sum(vis_re * zeta_im - vis_im * zeta_re, axis=-2)
    denom = jnp.sum(zeta_re * zeta_re + zeta_im * zeta_im, axis=-2)
    terms = jnp.stack([num_re, num_im, denom], axis=2) * flags.astype(jnp.float32)[..., None, None]
    summed = jnp.einsum("kbn,kbcr->kcnr", col_hot, terms, precision=lax.Precision.HIGHEST)
    return summed.reshape(count, 3, blocks * width)


def smooth_terms(terms, couplings):
    ftiles, ttiles = (terms.shape[0], terms.shape[1])
    cycle = extended(terms, (("freq", 0),), 2, True)
    line = extended(terms, (("tm", 1),), 1, False)
    later = line[:, 0:ttiles] + line[:, 2 : 2 + ttiles]
    near = cycle[1 : 1 + ftiles] + cycle[3 : 3 + ftiles]
    far = cycle[0:ftiles] + cycle[4 : 4 + ftiles]
    return terms + couplings[0] * near + couplings[1] * far + couplings[2] * later


def per_device(vis, model, block_rows, block_cols, flags, prior, couplings, damping):
    ftiles, ttiles = (prior.shape[0], prior.shape[1])
    count = ftiles * ttiles
    last_tile = shifted(prior[ftiles - 1 :], "freq", 1)
    prior_prev = jnp.concatenate([last_tile, prior[: ftiles - 1]], axis=0)
    flat_rows = block_rows.reshape(count, -1)
    flat_cols = block_cols.reshape(count, -1)
    flat_flags = flags.reshape(count, -1)
    flat_vis = vis.reshape((count,) + vis.shape[2:])
    flat_model = model.reshape((count,) + model.shape[2:])
    current = prior
    change_list = []
    scale_list = []
    for step in range(ITERS):
        terms = tile_terms(
            current.reshape(count, 2, -1), flat_rows, flat_cols, flat_flags, flat_vis, flat_model
        )
        smooth = smooth_terms(terms.reshape(ftiles, ttiles, 3, -1), couplings)
        numer = smooth[:, :, 0:2] + damping * prior_prev
        denom = smooth[:, :, 2] + damping
        fresh = numer / denom[:, :, None]
        if step % 2 == 1:
            fresh = 0.5 * (fresh + current)
        change = jnp.sum((fresh - current) ** 2)
        scale = jnp.sum(fresh * fresh)
        change_list.append(change)
        scale_list.append(scale)
        current = fresh
    change_all = jnp.stack(change_list)
    scale_all = jnp.stack(scale_list)
    change_all, scale_all = lax.psum((change_all, scale_all), ("freq", "tm"))
    return (current, jnp.sqrt(change_all / (scale_all + 1e-06)))


def solution(mesh):
    placed = (
        P("freq", "tm", None, None, None, None),
        P("freq", "tm", None, None, None, None),
        P("freq", "tm", None),
        P("freq", "tm", None),
        P("freq", "tm", None),
        P("freq", "tm", None, None),
        P(),
        P(),
    )
    return jax.shard_map(
        per_device,
        mesh=mesh,
        in_specs=placed,
        out_specs=(P("freq", "tm", None, None), P()),
        check_vma=False,
    )
```

profile of v0, /device:TPU:0, one launch (start us, length us, event | category | flops | bytes accessed | tf_op | source)
XLA Modules:
  0.0 135.2 jit_solution(2613959916976540886)
XLA Ops:
  0.6 0.7 convert_element_type.65
  1.3 0.9 reshape_reshape.24
  2.2 0.9 fusion.90
  3.2 7.7 %fusion.1 = (f32[4,16,128]{2,1,0:T(8,128)S(1)}, f32[4,16,128]{2,1,0:T(8,128)S(1)}, f32[4,16,128]{2,1,0:T(8,128)S(1)}) fusion(f32[4,16,128]{2,1,0:T(8,128)S(1)} %get-tuple-element.44, f32[4,16,128]{2,1,0:T(8,128)S(1)} %get-tuple-element.43, bf16[4,16,2,128,128]{4,3,2,1,0:T(8,128)(2,1)} %bitcast.197, bf16[4,16,2,128,128]{4,3,2,1,0:T(8,128)(2,1)} %bitcast.201), kind=kLoop, calls=%fused_computation.33 | loop fusion | flops 23044096 | bytes 8552448 | tf_op jit(solution)/shard_map/reduce_sum | solution.py:47
  10.9 0.3 convolution_bitcast_fusion.3
  11.2 6.1 %collective-permute-start.1 = (f32[2,2,3,2048]{3,1,0,2:T(2,128)S(1)}, f32[2,2,3,2048]{3,1,0,2:T(2,128)S(1)}, u32[]{:S(2)}, u32[]{:S(2)}) collective-permute-start(f32[2,2,3,2048]{3,1,0,2:T(2,128)S(1)} %reshape_reshape.25), channel_id=1, source_target_pairs={{4,0},{8,4},{12,8},{16,12},{20,16},{24,20},{28,24},{0,28},{5,1},{9... | collective-permute-start | bytes 294920 | tf_op jit(solution)/shard_map/ppermute | solution.py:19
  17.3 0.1 collective-permute-start.4
  17.4 0.1 fusion.114
  17.5 1.5 %collective-permute-start.2 = (f32[2,1,3,2048]{3,1,0,2:T(1,128)S(1)}, f32[2,1,3,2048]{3,1,0,2:T(1,128)S(1)}, u32[]{:S(2)}, u32[]{:S(2)}) collective-permute-start(f32[2,1,3,2048]{3,1,0,2:T(1,128)S(1)} %get-tuple-element.33), channel_id=1, source_target_pairs={{0,1},{1,2},{2,3},{4,5},{5,6},{6,7},{8,9},{9,10},{10,11},{12,13},{... | collective-permute-start | bytes 147464 | tf_op jit(solution)/shard_map/ppermute | solution.py:16
  19.0 1.3 collective-permute-start.3
  20.3 3.3 %collective-permute-done.3 = f32[2,1,3,2048]{3,1,0,2:T(1,128)S(1)} collective-permute-done((f32[2,1,3,2048]{3,1,0,2:T(1,128)S(1)}, f32[2,1,3,2048]{3,1,0,2:T(1,128)S(1)}, u32[]{:S(2)}, u32[]{:S(2)}) %collective-permute-start.3) | collective-permute-done | bytes 49184 | tf_op jit(solution)/shard_map/ppermute | solution.py:19
  23.7 0.9 collective-permute-done
  24.6 0.3 fusion.47
  25.0 0.1 fusion.69
  25.1 0.2 fusion.74
  25.3 7.7 %fusion.5 = (f32[4,16,128]{2,1,0:T(8,128)S(1)}, f32[4,16,128]{2,1,0:T(8,128)S(1)}, f32[4,16,128]{2,1,0:T(8,128)S(1)}) fusion(f32[4,16,128]{2,1,0:T(8,128)S(1)} %get-tuple-element.40, f32[4,16,128]{2,1,0:T(8,128)S(1)} %get-tuple-element.39, bf16[4,16,2,128,128]{4,3,2,1,0:T(8,128)(2,1)} %bitcast.198, bf16[4,16,2,128,128]{4,3,2,1,0:T(8,128)(2,1)} %bitcast.202), kind=kLoop, calls=%fused_computation.37 | loop fusion | flops 23044096 | bytes 8552448 | tf_op jit(solution)/shard_map/reduce_sum | solution.py:47
  33.0 0.2 convolution_bitcast_fusion.2
  33.3 3.8 %collective-permute-start.6 = (f32[2,2,3,2048]{3,1,0,2:T(2,128)S(1)}, f32[2,2,3,2048]{3,1,0,2:T(2,128)S(1)}, u32[]{:S(2)}, u32[]{:S(2)}) collective-permute-start(f32[2,2,3,2048]{3,1,0,2:T(2,128)S(1)} %reshape_reshape.27), channel_id=1, source_target_pairs={{4,0},{8,4},{12,8},{16,12},{20,16},{24,20},{28,24},{0,28},{5,1},{9... | collective-permute-start | bytes 294920 | tf_op jit(solution)/shard_map/ppermute | solution.py:19
  37.2 0.1 fusion.113
  37.3 4.4 %collective-permute-start.7 = (f32[2,1,3,2048]{3,1,0,2:T(1,128)S(1)}, f32[2,1,3,2048]{3,1,0,2:T(1,128)S(1)}, u32[]{:S(2)}, u32[]{:S(2)}) collective-permute-start(f32[2,1,3,2048]{3,1,0,2:T(1,128)S(1)} %get-tuple-element.31), channel_id=1, source_target_pairs={{0,1},{1,2},{2,3},{4,5},{5,6},{6,7},{8,9},{9,10},{10,11},{12,13},{... | collective-permute-start | bytes 147464 | tf_op jit(solution)/shard_map/ppermute | solution.py:16
  41.7 1.3 collective-permute-start.8
  43.0 1.8 %collective-permute-done.8 = f32[2,1,3,2048]{3,1,0,2:T(1,128)S(1)} collective-permute-done((f32[2,1,3,2048]{3,1,0,2:T(1,128)S(1)}, f32[2,1,3,2048]{3,1,0,2:T(1,128)S(1)}, u32[]{:S(2)}, u32[]{:S(2)}) %collective-permute-start.8) | collective-permute-done | bytes 49184 | tf_op jit(solution)/shard_map/ppermute | solution.py:19
  44.8 0.3 fusion.40
  45.1 0.1 fusion.76
  45.3 0.2 fusion.72
  45.5 7.7 %fusion.9 = (f32[4,16,128]{2,1,0:T(8,128)S(1)}, f32[4,16,128]{2,1,0:T(8,128)S(1)}, f32[4,16,128]{2,1,0:T(8,128)S(1)}) fusion(f32[4,16,128]{2,1,0:T(8,128)S(1)} %get-tuple-element.38, f32[4,16,128]{2,1,0:T(8,128)S(1)} %get-tuple-element.37, bf16[4,16,2,128,128]{4,3,2,1,0:T(8,128)(2,1)} %bitcast.199, bf16[4,16,2,128,128]{4,3,2,1,0:T(8,128)(2,1)} %bitcast.203), kind=kLoop, calls=%fused_computation.41 | loop fusion | flops 23044096 | bytes 8552448 | tf_op jit(solution)/shard_map/reduce_sum | solution.py:47
  53.2 0.3 convolution_bitcast_fusion.1
  53.6 4.5 %collective-permute-start.10 = (f32[2,2,3,2048]{3,1,0,2:T(2,128)S(1)}, f32[2,2,3,2048]{3,1,0,2:T(2,128)S(1)}, u32[]{:S(2)}, u32[]{:S(2)}) collective-permute-start(f32[2,2,3,2048]{3,1,0,2:T(2,128)S(1)} %reshape_reshape.29), channel_id=1, source_target_pairs={{4,0},{8,4},{12,8},{16,12},{20,16},{24,20},{28,24},{0,28},{5,1},{9... | collective-permute-start | bytes 294920 | tf_op jit(solution)/shard_map/ppermute | solution.py:19
  58.1 0.1 fusion.112
  58.2 4.4 %collective-permute-start.11 = (f32[2,1,3,2048]{3,1,0,2:T(1,128)S(1)}, f32[2,1,3,2048]{3,1,0,2:T(1,128)S(1)}, u32[]{:S(2)}, u32[]{:S(2)}) collective-permute-start(f32[2,1,3,2048]{3,1,0,2:T(1,128)S(1)} %get-tuple-element.29), channel_id=1, source_target_pairs={{0,1},{1,2},{2,3},{4,5},{5,6},{6,7},{8,9},{9,10},{10,11},{12,13},{... | collective-permute-start | bytes 147464 | tf_op jit(solution)/shard_map/ppermute | solution.py:16
  62.6 1.3 collective-permute-start.12
  63.9 1.8 %collective-permute-done.12 = f32[2,1,3,2048]{3,1,0,2:T(1,128)S(1)} collective-permute-done((f32[2,1,3,2048]{3,1,0,2:T(1,128)S(1)}, f32[2,1,3,2048]{3,1,0,2:T(1,128)S(1)}, u32[]{:S(2)}, u32[]{:S(2)}) %collective-permute-start.12) | collective-permute-done | bytes 49184 | tf_op jit(solution)/shard_map/ppermute | solution.py:19
  65.7 0.3 fusion.33
  66.1 0.1 fusion.68
  66.2 0.2 fusion.70
  66.4 7.7 %fusion.13 = (f32[4,16,128]{2,1,0:T(8,128)S(1)}, f32[4,16,128]{2,1,0:T(8,128)S(1)}, f32[4,16,128]{2,1,0:T(8,128)S(1)}) fusion(f32[4,16,128]{2,1,0:T(8,128)S(1)} %get-tuple-element.36, f32[4,16,128]{2,1,0:T(8,128)S(1)} %get-tuple-element.35, bf16[4,16,2,128,128]{4,3,2,1,0:T(8,128)(2,1)} %bitcast.200, bf16[4,16,2,128,128]{4,3,2,1,0:T(8,128)(2,1)} %bitcast.204), kind=kLoop, calls=%fused_computation.45 | loop fusion | flops 23044096 | bytes 8552448 | tf_op jit(solution)/shard_map/reduce_sum | solution.py:47
  74.1 0.2 convolution_bitcast_fusion
  74.4 4.5 %collective-permute-start.14 = (f32[2,2,3,2048]{3,1,0,2:T(2,128)S(1)}, f32[2,2,3,2048]{3,1,0,2:T(2,128)S(1)}, u32[]{:S(2)}, u32[]{:S(2)}) collective-permute-start(f32[2,2,3,2048]{3,1,0,2:T(2,128)S(1)} %reshape_reshape.31), channel_id=1, source_target_pairs={{4,0},{8,4},{12,8},{16,12},{20,16},{24,20},{28,24},{0,28},{5,1},{9... | collective-permute-start | bytes 294920 | tf_op jit(solution)/shard_map/ppermute | solution.py:19
  79.0 0.1 fusion.111
  79.1 4.4 %collective-permute-start.15 = (f32[2,1,3,2048]{3,1,0,2:T(1,128)S(1)}, f32[2,1,3,2048]{3,1,0,2:T(1,128)S(1)}, u32[]{:S(2)}, u32[]{:S(2)}) collective-permute-start(f32[2,1,3,2048]{3,1,0,2:T(1,128)S(1)} %get-tuple-element.27), channel_id=1, source_target_pairs={{0,1},{1,2},{2,3},{4,5},{5,6},{6,7},{8,9},{9,10},{10,11},{12,13},{... | collective-permute-start | bytes 147464 | tf_op jit(solution)/shard_map/ppermute | solution.py:16
  83.5 1.3 collective-permute-start.16
  84.8 1.8 %collective-permute-done.16 = f32[2,1,3,2048]{3,1,0,2:T(1,128)S(1)} collective-permute-done((f32[2,1,3,2048]{3,1,0,2:T(1,128)S(1)}, f32[2,1,3,2048]{3,1,0,2:T(1,128)S(1)}, u32[]{:S(2)}, u32[]{:S(2)}) %collective-permute-start.16) | collective-permute-done | bytes 49184 | tf_op jit(solution)/shard_map/ppermute | solution.py:19
  86.6 0.3 fusion.26
  86.9 1.0 multiply_reduce_fusion.3
  88.0 0.7 copy.26
  88.6 5.0 %pad_maximum_fusion.16 = (f32[4]{0:T(128)S(1)}, f32[4]{0:T(128)S(1)}) fusion(f32[1]{0:T(128)} %bitcast.52, f32[1]{0:T(128)} %bitcast.51, f32[1]{0:T(128)} %bitcast.50, f32[1]{0:T(128)} %bitcast.49, f32[1]{0:T(128)} %bitcast.56, f32[1]{0:T(128)} %bitcast.55, f32[1]{0:T(128)} %bitcast.54, f32[1]{0:T(128)} %bitcast.53), kind=kLoop, calls=%fused_computation.190 | loop fusion | flops 24 | bytes 64 | tf_op jit(solution)/shard_map/stack | solution.py:93
  93.7 41.1 %all-reduce = (f32[4]{0:T(128)S(1)}, f32[4]{0:T(128)S(1)}) all-reduce(f32[4]{0:T(128)S(1)} %get-tuple-element.48, f32[4]{0:T(128)S(1)} %get-tuple-element.49), channel_id=1, replica_groups=mesh['freq'=8,'tm'=4] {'freq','tm'}, use_global_device_ids=true, to_apply=%region_16.0 | all-reduce | flops 8 | bytes 64 | tf_op jit(solution)/shard_map/psum | solution.py:95
  134.7 0.5 fusion.105
  (49 shorter events, 0.7 us)
Async XLA Ops:
  3.1 7.8 %copy-start.3 = (s32[2,2,16]{2,1,0:T(2,128)S(1)}, s32[2,2,16]{2,1,0:T(2,128)}, u32[]{:S(2)}) copy-start(s32[2,2,16]{2,1,0:T(2,128)} %param.11) | copy-start | bytes 772
  3.1 14.1 %copy-start = (f32[2,2,2,2048]{3,2,1,0:T(2,128)S(1)}, f32[2,2,2,2048]{3,2,1,0:T(2,128)}, u32[]{:S(2)}) copy-start(f32[2,2,2,2048]{3,2,1,0:T(2,128)} %param.13) | copy-start | bytes 196612
  3.2 17.1 %copy-start.4 = (f32[3,2048]{1,0:T(4,128)S(1)}, f32[3,2048]{1,0:T(4,128)}, u32[]{:S(2)}) copy-start(f32[3,2048]{1,0:T(4,128)} %param.14) | copy-start | bytes 73732
  3.2 21.7 %copy-start.1 = (f32[2048]{0:T(1024)S(1)}, f32[2048]{0:T(1024)}, u32[]{:S(2)}) copy-start(f32[2048]{0:T(1024)} %param.15) | copy-start | bytes 24580
  3.2 21.9 %copy-start.2 = (s32[2,2,16]{2,1,0:T(2,128)S(1)}, s32[2,2,16]{2,1,0:T(2,128)}, u32[]{:S(2)}) copy-start(s32[2,2,16]{2,1,0:T(2,128)} %param.10) | copy-start | bytes 772
  11.2 12.4 %collective-permute-start.1 = (f32[2,2,3,2048]{3,1,0,2:T(2,128)S(1)}, f32[2,2,3,2048]{3,1,0,2:T(2,128)S(1)}, u32[]{:S(2)}, u32[]{:S(2)}) collective-permute-start(f32[2,2,3,2048]{3,1,0,2:T(2,128)S(1)} %reshape_reshape.25), channel_id=1, source_target_pairs={{4,0},{8,4},{12,8},{16,12},{20,16},{24,20},{28,24},{0,28},{5,1},{9... | collective-permute-start | bytes 294920 | tf_op jit(solution)/shard_map/ppermute | solution.py:19
  17.3 7.3 %collective-permute-start = (f32[2,2,3,2048]{3,1,0,2:T(2,128)S(1)}, f32[2,2,3,2048]{3,1,0,2:T(2,128)S(1)}, u32[]{:S(2)}, u32[]{:S(2)}) collective-permute-start(f32[2,2,3,2048]{3,1,0,2:T(2,128)S(1)} %reshape_reshape.25), channel_id=1, source_target_pairs={{0,4},{4,8},{8,12},{12,16},{16,20},{20,24},{24,28},{28,0},{1,5},{5... | collective-permute-start | bytes 294920 | tf_op jit(solution)/shard_map/ppermute | solution.py:16
  17.3 7.6 %collective-permute-start.4 = (f32[1,2,2,2048]{3,1,0,2:T(2,128)S(1)}, f32[1,2,2,2048]{3,1,0,2:T(2,128)S(1)}, u32[]{:S(2)}, u32[]{:S(2)}) collective-permute-start(f32[1,2,2,2048]{3,1,0,2:T(2,128)S(1)} %copy.40), channel_id=1, source_target_pairs={{0,4},{4,8},{8,12},{12,16},{16,20},{20,24},{24,28},{28,0},{1,5},{5... | collective-permute-start | bytes 98312 | tf_op jit(solution)/shard_map/ppermute | solution.py:27
  17.5 2.8 %collective-permute-start.2 = (f32[2,1,3,2048]{3,1,0,2:T(1,128)S(1)}, f32[2,1,3,2048]{3,1,0,2:T(1,128)S(1)}, u32[]{:S(2)}, u32[]{:S(2)}) collective-permute-start(f32[2,1,3,2048]{3,1,0,2:T(1,128)S(1)} %get-tuple-element.33), channel_id=1, source_target_pairs={{0,1},{1,2},{2,3},{4,5},{5,6},{6,7},{8,9},{9,10},{10,11},{12,13},{... | collective-permute-start | bytes 147464 | tf_op jit(solution)/shard_map/ppermute | solution.py:16
  19.0 4.7 %collective-permute-start.3 = (f32[2,1,3,2048]{3,1,0,2:T(1,128)S(1)}, f32[2,1,3,2048]{3,1,0,2:T(1,128)S(1)}, u32[]{:S(2)}, u32[]{:S(2)}) collective-permute-start(f32[2,1,3,2048]{3,1,0,2:T(1,128)S(1)} %get-tuple-element.34), channel_id=1, source_target_pairs={{1,0},{2,1},{3,2},{5,4},{6,5},{7,6},{9,8},{10,9},{11,10},{13,12},{... | collective-permute-start | bytes 147464 | tf_op jit(solution)/shard_map/ppermute | solution.py:19
  33.3 11.5 %collective-permute-start.6 = (f32[2,2,3,2048]{3,1,0,2:T(2,128)S(1)}, f32[2,2,3,2048]{3,1,0,2:T(2,128)S(1)}, u32[]{:S(2)}, u32[]{:S(2)}) collective-permute-start(f32[2,2,3,2048]{3,1,0,2:T(2,128)S(1)} %reshape_reshape.27), channel_id=1, source_target_pairs={{4,0},{8,4},{12,8},{16,12},{20,16},{24,20},{28,24},{0,28},{5,1},{9... | collective-permute-start | bytes 294920 | tf_op jit(solution)/shard_map/ppermute | solution.py:19
  37.2 7.6 %collective-permute-start.5 = (f32[2,2,3,2048]{3,1,0,2:T(2,128)S(1)}, f32[2,2,3,2048]{3,1,0,2:T(2,128)S(1)}, u32[]{:S(2)}, u32[]{:S(2)}) collective-permute-start(f32[2,2,3,2048]{3,1,0,2:T(2,128)S(1)} %reshape_reshape.27), channel_id=1, source_target_pairs={{0,4},{4,8},{8,12},{12,16},{16,20},{20,24},{24,28},{28,0},{1,5},{5... | collective-permute-start | bytes 294920 | tf_op jit(solution)/shard_map/ppermute | solution.py:16
  37.3 5.7 %collective-permute-start.7 = (f32[2,1,3,2048]{3,1,0,2:T(1,128)S(1)}, f32[2,1,3,2048]{3,1,0,2:T(1,128)S(1)}, u32[]{:S(2)}, u32[]{:S(2)}) collective-permute-start(f32[2,1,3,2048]{3,1,0,2:T(1,128)S(1)} %get-tuple-element.31), channel_id=1, source_target_pairs={{0,1},{1,2},{2,3},{4,5},{5,6},{6,7},{8,9},{9,10},{10,11},{12,13},{... | collective-permute-start | bytes 147464 | tf_op jit(solution)/shard_map/ppermute | solution.py:16
  41.7 3.1 %collective-permute-start.8 = (f32[2,1,3,2048]{3,1,0,2:T(1,128)S(1)}, f32[2,1,3,2048]{3,1,0,2:T(1,128)S(1)}, u32[]{:S(2)}, u32[]{:S(2)}) collective-permute-start(f32[2,1,3,2048]{3,1,0,2:T(1,128)S(1)} %get-tuple-element.32), channel_id=1, source_target_pairs={{1,0},{2,1},{3,2},{5,4},{6,5},{7,6},{9,8},{10,9},{11,10},{13,12},{... | collective-permute-start | bytes 147464 | tf_op jit(solution)/shard_map/ppermute | solution.py:19
  53.6 12.2 %collective-permute-start.10 = (f32[2,2,3,2048]{3,1,0,2:T(2,128)S(1)}, f32[2,2,3,2048]{3,1,0,2:T(2,128)S(1)}, u32[]{:S(2)}, u32[]{:S(2)}) collective-permute-start(f32[2,2,3,2048]{3,1,0,2:T(2,128)S(1)} %reshape_reshape.29), channel_id=1, source_target_pairs={{4,0},{8,4},{12,8},{16,12},{20,16},{24,20},{28,24},{0,28},{5,1},{9... | collective-permute-start | bytes 294920 | tf_op jit(solution)/shard_map/ppermute | solution.py:19
  58.1 7.6 %collective-permute-start.9 = (f32[2,2,3,2048]{3,1,0,2:T(2,128)S(1)}, f32[2,2,3,2048]{3,1,0,2:T(2,128)S(1)}, u32[]{:S(2)}, u32[]{:S(2)}) collective-permute-start(f32[2,2,3,2048]{3,1,0,2:T(2,128)S(1)} %reshape_reshape.29), channel_id=1, source_target_pairs={{0,4},{4,8},{8,12},{12,16},{16,20},{20,24},{24,28},{28,0},{1,5},{5... | collective-permute-start | bytes 294920 | tf_op jit(solution)/shard_map/ppermute | solution.py:16
  58.2 5.7 %collective-permute-start.11 = (f32[2,1,3,2048]{3,1,0,2:T(1,128)S(1)}, f32[2,1,3,2048]{3,1,0,2:T(1,128)S(1)}, u32[]{:S(2)}, u32[]{:S(2)}) collective-permute-start(f32[2,1,3,2048]{3,1,0,2:T(1,128)S(1)} %get-tuple-element.29), channel_id=1, source_target_pairs={{0,1},{1,2},{2,3},{4,5},{5,6},{6,7},{8,9},{9,10},{10,11},{12,13},{... | collective-permute-start | bytes 147464 | tf_op jit(solution)/shard_map/ppermute | solution.py:16
  62.6 3.1 %collective-permute-start.12 = (f32[2,1,3,2048]{3,1,0,2:T(1,128)S(1)}, f32[2,1,3,2048]{3,1,0,2:T(1,128)S(1)}, u32[]{:S(2)}, u32[]{:S(2)}) collective-permute-start(f32[2,1,3,2048]{3,1,0,2:T(1,128)S(1)} %get-tuple-element.30), channel_id=1, source_target_pairs={{1,0},{2,1},{3,2},{5,4},{6,5},{7,6},{9,8},{10,9},{11,10},{13,12},{... | collective-permute-start | bytes 147464 | tf_op jit(solution)/shard_map/ppermute | solution.py:19
  74.4 12.2 %collective-permute-start.14 = (f32[2,2,3,2048]{3,1,0,2:T(2,128)S(1)}, f32[2,2,3,2048]{3,1,0,2:T(2,128)S(1)}, u32[]{:S(2)}, u32[]{:S(2)}) collective-permute-start(f32[2,2,3,2048]{3,1,0,2:T(2,128)S(1)} %reshape_reshape.31), channel_id=1, source_target_pairs={{4,0},{8,4},{12,8},{16,12},{20,16},{24,20},{28,24},{0,28},{5,1},{9... | collective-permute-start | bytes 294920 | tf_op jit(solution)/shard_map/ppermute | solution.py:19
  79.0 7.6 %collective-permute-start.13 = (f32[2,2,3,2048]{3,1,0,2:T(2,128)S(1)}, f32[2,2,3,2048]{3,1,0,2:T(2,128)S(1)}, u32[]{:S(2)}, u32[]{:S(2)}) collective-permute-start(f32[2,2,3,2048]{3,1,0,2:T(2,128)S(1)} %reshape_reshape.31), channel_id=1, source_target_pairs={{0,4},{4,8},{8,12},{12,16},{16,20},{20,24},{24,28},{28,0},{1,5},{5... | collective-permute-start | bytes 294920 | tf_op jit(solution)/shard_map/ppermute | solution.py:16
  79.1 5.7 %collective-permute-start.15 = (f32[2,1,3,2048]{3,1,0,2:T(1,128)S(1)}, f32[2,1,3,2048]{3,1,0,2:T(1,128)S(1)}, u32[]{:S(2)}, u32[]{:S(2)}) collective-permute-start(f32[2,1,3,2048]{3,1,0,2:T(1,128)S(1)} %get-tuple-element.27), channel_id=1, source_target_pairs={{0,1},{1,2},{2,3},{4,5},{5,6},{6,7},{8,9},{9,10},{10,11},{12,13},{... | collective-permute-start | bytes 147464 | tf_op jit(solution)/shard_map/ppermute | solution.py:16
  83.5 3.1 %collective-permute-start.16 = (f32[2,1,3,2048]{3,1,0,2:T(1,128)S(1)}, f32[2,1,3,2048]{3,1,0,2:T(1,128)S(1)}, u32[]{:S(2)}, u32[]{:S(2)}) collective-permute-start(f32[2,1,3,2048]{3,1,0,2:T(1,128)S(1)} %get-tuple-element.28), channel_id=1, source_target_pairs={{1,0},{2,1},{3,2},{5,4},{6,5},{7,6},{9,8},{10,9},{11,10},{13,12},{... | collective-permute-start | bytes 147464 | tf_op jit(solution)/shard_map/ppermute | solution.py:19
where the time goes:
time: 136 us; the launch traced here: 135 us
  blocking collectives  41.1 us (30%)
  other arithmetic  39.4 us (29%)
  starting transfers between devices  38.9 us (29%)
  waiting for transfers between devices  9.75 us (7%)
  matrix products  2.56 us (2%)
  local copies, waits for them, and re-layouts  2.42 us (2%)
    psum x1, blocking collectives, per_device(): change_all, scale_all = lax.psum((change_all, scale_all), ('freq', 'tm'))  41.1 us
    reduce_sum x4, other arithmetic, tile_terms(): num_re = jnp.sum(vis_re * zeta_re + vis_im * zeta_im, axis=-2)  30.7 us
    ppermute x8, starting transfers between devices, extended(): lax.ppermute(lax.slice_in_dim(block, 0, width, axis=dim), axis, backward)  24.1 us
    ppermute x8, starting transfers between devices, extended(): lax.ppermute(lax.slice_in_dim(block, block.shape[dim] - width, None, axis...  14.7 us
    ppermute x8, waiting for transfers between devices, extended(): lax.ppermute(lax.slice_in_dim(block, 0, width, axis=dim), axis, backward)  8.78 us
    another operation x1, other arithmetic, per_device(): change_all = jnp.stack(change_list)  5.01 us
  transfers between devices with their start and end apart: 17, of which 5 were waited for; matrix products, arithmetic and copies ran while one was open for 1% of the time, Pallas kernels for 0%

commit v1 on v0

v1 whole, which is shorter than its diff:
```python
import functools

import jax
import jax.numpy as jnp
from jax import lax
from jax.experimental import pallas as pl
from jax.experimental.pallas import tpu as pltpu
from jax.sharding import PartitionSpec as P

ITERS = 4
REACH = 2
MESH = pl.DeviceIdType.MESH
F32 = jnp.float32
BF16 = jnp.bfloat16


def split(value):
    high = value.astype(BF16)
    return high, (value - high.astype(F32)).astype(BF16)


def kernel(
    dims,
    vis_ref, model_ref, rows_ref, cols_ref, flags_ref, prior_ref, coup_ref, damp_ref,
    gains_ref, changes_ref,
    vbuf, mbuf, wa, wb, gain, prev, coef, from_prior, terms, low, high, early, late,
    stats, all_freq, part, all_tm,
    load_sem, prior_sem, up_send, down_send, low_recv, high_recv,
    early_send, late_send, early_recv, late_recv, freq_send, freq_recv, tm_send, tm_recv,
):
    nf, nt, ftiles, ttiles, blks, width, nb = dims
    fi = lax.axis_index("freq")
    ti = lax.axis_index("tm")
    above, below = lax.rem(fi + 1, nf), lax.rem(fi + nf - 1, nf)
    tiles = [(f, t) for f in range(ftiles) for t in range(ttiles)]

    barrier = pltpu.get_barrier_semaphore()
    for step in range(1, nf):
        pl.semaphore_signal(
            barrier, inc=1, device_id={"freq": lax.rem(fi + step, nf)}, device_id_type=MESH
        )
    for step in range(1, nt):
        pl.semaphore_signal(
            barrier, inc=1, device_id={"tm": lax.rem(ti + step, nt)}, device_id_type=MESH
        )

    def loads(f, t):
        i = f * ttiles + t
        return (
            pltpu.make_async_copy(vis_ref.at[f, t], vbuf.at[i], load_sem.at[0, i]),
            pltpu.make_async_copy(model_ref.at[f, t], mbuf.at[i], load_sem.at[1, i]),
        )

    for f, t in tiles:
        for copy in loads(f, t):
            copy.start()

    for f, t in tiles:
        i = f * ttiles + t
        for c in range(2):
            for n in range(nb):
                gain[i, c, n : n + 1, :] = prior_ref[f, t, c : c + 1, n * width : (n + 1) * width]
    for n in range(nb):
        for c in range(3):
            coef[c, n : n + 1, :] = coup_ref[c : c + 1, n * width : (n + 1) * width]
        coef[3, n : n + 1, :] = damp_ref[0:1, n * width : (n + 1) * width]

    @pl.when(ti == 0)
    def _():
        early[...] = jnp.zeros_like(early)

    @pl.when(ti == nt - 1)
    def _():
        late[...] = jnp.zeros_like(late)

    pl.semaphore_wait(barrier, nf - 1 + nt - 1)

    prior_copy = pltpu.make_async_remote_copy(
        src_ref=prior_ref.at[ftiles - 1], dst_ref=from_prior,
        send_sem=prior_sem.at[0], recv_sem=prior_sem.at[1],
        device_id={"freq": above}, device_id_type=MESH,
    )
    prior_copy.start()

    def up_copy(k, f, t):
        s = (f - (ftiles - REACH)) * ttiles + t
        return pltpu.make_async_remote_copy(
            src_ref=terms.at[k, f * ttiles + t], dst_ref=low.at[k, s],
            send_sem=up_send.at[k, s], recv_sem=low_recv.at[k, s],
            device_id={"freq": above}, device_id_type=MESH,
        )

    def down_copy(k, f, t):
        s = f * ttiles + t
        return pltpu.make_async_remote_copy(
            src_ref=terms.at[k, f * ttiles + t], dst_ref=high.at[k, s],
            send_sem=down_send.at[k, s], recv_sem=high_recv.at[k, s],
            device_id={"freq": below}, device_id_type=MESH,
        )

    def later_copy(k, f):
        return pltpu.make_async_remote_copy(
            src_ref=terms.at[k, f * ttiles + ttiles - 1], dst_ref=early.at[k, f],
            send_sem=early_send.at[k, f], recv_sem=early_recv.at[k, f],
            device_id={"tm": jnp.minimum(ti + 1, nt - 1)}, device_id_type=MESH,
        )

    def earlier_copy(k, f):
        return pltpu.make_async_remote_copy(
            src_ref=terms.at[k, f * ttiles], dst_ref=late.at[k, f],
            send_sem=late_send.at[k, f], recv_sem=late_recv.at[k, f],
            device_id={"tm": jnp.maximum(ti - 1, 0)}, device_id_type=MESH,
        )

    def prepare(i):
        def one(b, carry):
            v_re = vbuf[i, b, 0].astype(F32)
            v_im = vbuf[i, b, 1].astype(F32)
            m_re = mbuf[i, b, 0].astype(F32)
            m_im = mbuf[i, b, 1].astype(F32)
            re_hi, re_lo = split(v_re * m_re + v_im * m_im)
            im_hi, im_lo = split(v_re * m_im - v_im * m_re)
            sq_hi, sq_lo = split(m_re * m_re + m_im * m_im)
            wa[i * blks + b, 0:width, 0:width] = re_hi
            wa[i * blks + b, width:, 0:width] = im_hi
            wa[i * blks + b, 0:width, width:] = sq_hi
            wa[i * blks + b, width:, width:] = sq_lo
            wb[i * blks + b, 0:width, :] = re_lo
            wb[i * blks + b, width:, :] = im_lo
            return carry

        lax.fori_loop(0, blks, one, 0)

    row_of = lax.broadcasted_iota(jnp.int32, (8, width), 0)
    block_of = lax.broadcasted_iota(jnp.int32, (nb, width), 0)

    def tile_terms(k, f, t):
        i = f * ttiles + t
        total = [jnp.zeros((nb, width), F32) for _ in range(3)]
        for b in range(blks):
            row = rows_ref[f, t, b]
            col = jnp.where(flags_ref[f, t, b] != 0, cols_ref[f, t, b], -1)
            re = jnp.broadcast_to(gain[i, 0, pl.ds(row, 1), :], (8, width))
            im = jnp.broadcast_to(gain[i, 1, pl.ds(row, 1), :], (8, width))
            sq = re * re + im * im
            left = jnp.where(row_of == 0, re, jnp.where(row_of == 1, im, sq))
            right = jnp.where(row_of == 0, -im, jnp.where(row_of == 1, re, sq))
            lhs = jnp.concatenate([left, right], axis=1)
            lhs_hi = lhs.astype(BF16).astype(F32)
            lhs = jnp.concatenate([lhs_hi, lhs - lhs_hi], axis=0).astype(BF16)
            out_a = jnp.dot(lhs, wa[i * blks + b], preferred_element_type=F32)
            out_b = jnp.dot(lhs, wb[i * blks + b], preferred_element_type=F32)
            out_a = out_a[0:8] + out_a[8:16]
            num = out_a[:, 0:width] + (out_b[0:8] + out_b[8:16])
            den = out_a[:, width:]
            hit = block_of == col
            parts = (num[0:1], num[1:2], den[2:3])
            total = [
                acc + jnp.where(hit, jnp.broadcast_to(one, (nb, width)), 0.0)
                for acc, one in zip(total, parts)
            ]
        for c in range(3):
            terms[k, i, c] = total[c]

    def iteration(k, carry):
        for f, t in tiles:
            i = f * ttiles + t

            @pl.when(k == 0)
            def _():
                for copy in loads(f, t):
                    copy.wait()
                prepare(i)

            tile_terms(k, f, t)
            if f >= ftiles - REACH:
                up_copy(k, f, t).start()
            if f < REACH:
                down_copy(k, f, t).start()
            if t == ttiles - 1:
                @pl.when(ti < nt - 1)
                def _():
                    later_copy(k, f).start()
            if t == 0:
                @pl.when(ti > 0)
                def _():
                    earlier_copy(k, f).start()

        @pl.when(k == 0)
        def _():
            prior_copy.wait_recv()
            for f, t in tiles:
                i = f * ttiles + t
                for c in range(2):
                    if f == 0:
                        for n in range(nb):
                            prev[i, c, n : n + 1, :] = from_prior[
                                t, c : c + 1, n * width : (n + 1) * width
                            ]
                        prev[i, c] = prev[i, c] * coef[3]
                    else:
                        prev[i, c] = gain[i - ttiles, c] * coef[3]

        for f in range(ftiles):
            @pl.when(ti > 0)
            def _():
                later_copy(k, f).wait_recv()

            @pl.when(ti < nt - 1)
            def _():
                earlier_copy(k, f).wait_recv()

        for f in range(ftiles - REACH, ftiles):
            for t in range(ttiles):
                up_copy(k, f, t).wait_recv()
        for f in range(REACH):
            for t in range(ttiles):
                down_copy(k, f, t).wait_recv()

        def at(f, t, c):
            if t < 0:
                return early[k, f, c]
            if t >= ttiles:
                return late[k, f, c]
            if f < 0:
                return low[k, (f + REACH) * ttiles + t, c]
            if f >= ftiles:
                return high[k, (f - ftiles) * ttiles + t, c]
            return terms[k, f * ttiles + t, c]

        odd = lax.rem(k, 2) == 1
        change = jnp.zeros((nb, width), F32)
        scale = jnp.zeros((nb, width), F32)
        for f, t in tiles:
            i = f * ttiles + t
            sums = [
                at(f, t, c)
                + coef[0] * (at(f - 1, t, c) + at(f + 1, t, c))
                + coef[1] * (at(f - 2, t, c) + at(f + 2, t, c))
                + coef[2] * (at(f, t - 1, c) + at(f, t + 1, c))
                for c in range(3)
            ]
            denom = sums[2] + coef[3]
            for c in range(2):
                old = gain[i, c]
                fresh = (sums[c] + prev[i, c]) / denom
                fresh = jnp.where(odd, 0.5 * (fresh + old), fresh)
                diff = fresh - old
                change = change + diff * diff
                scale = scale + fresh * fresh
                gain[i, c] = fresh
        stats[pl.ds(k, 1), :] = jnp.sum(change, axis=0, keepdims=True)
        stats[pl.ds(k + ITERS, 1), :] = jnp.sum(scale, axis=0, keepdims=True)
        return carry

    lax.fori_loop(0, ITERS, iteration, 0)

    def spread(axis, me, count, src, dst, send, recv):
        copies = [
            pltpu.make_async_remote_copy(
                src_ref=src, dst_ref=dst.at[me], send_sem=send.at[step], recv_sem=recv.at[me],
                device_id={axis: lax.rem(me + step, count)}, device_id_type=MESH,
            )
            for step in range(1, count)
        ]
        for copy in copies:
            copy.start()
        dst[me] = src[...]
        return copies

    def gathered(axis, me, count, src, dst, send, recv):
        for step in range(1, count):
            other = lax.rem(me + step, count)
            pltpu.make_async_remote_copy(
                src_ref=src, dst_ref=dst.at[other], send_sem=send.at[step],
                recv_sem=recv.at[other], device_id={axis: other}, device_id_type=MESH,
            ).wait_recv()
        return functools.reduce(lambda a, b: a + b, [dst[s] for s in range(count)])

    first = ("freq", fi, nf, stats, all_freq, freq_send, freq_recv)
    sent = spread(*first)
    for f, t in tiles:
        i = f * ttiles + t
        for c in range(2):
            for n in range(nb):
                gains_ref[f, t, c : c + 1, n * width : (n + 1) * width] = gain[i, c, n : n + 1, :]
    part[...] = gathered(*first)
    second = ("tm", ti, nt, part, all_tm, tm_send, tm_recv)
    sent += spread(*second)

    def drain(k, carry):
        for f, t in tiles:
            if f >= ftiles - REACH:
                up_copy(k, f, t).wait_send()
            if f < REACH:
                down_copy(k, f, t).wait_send()
        for f in range(ftiles):
            @pl.when(ti < nt - 1)
            def _():
                later_copy(k, f).wait_send()

            @pl.when(ti > 0)
            def _():
                earlier_copy(k, f).wait_send()
        return carry

    lax.fori_loop(0, ITERS, drain, 0)
    prior_copy.wait_send()
    whole = jnp.sum(gathered(*second), axis=1, keepdims=True)
    for copy in sent:
        copy.wait_send()
    ratio = jnp.sqrt(whole[0:ITERS] / (whole[ITERS : 2 * ITERS] + 1e-06))
    changes_ref[...] = jnp.broadcast_to(ratio, (ITERS, width))


def per_device(vis, model, block_rows, block_cols, flags, prior, couplings, damping):
    nf, nt = lax.axis_size("freq"), lax.axis_size("tm")
    ftiles, ttiles, blks = vis.shape[:3]
    width = vis.shape[-1]
    nb = prior.shape[-1] // width
    count = ftiles * ttiles
    dims = (nf, nt, ftiles, ttiles, blks, width, nb)
    vmem = pl.BlockSpec(memory_space=pltpu.VMEM)
    smem = pl.BlockSpec(memory_space=pltpu.SMEM)
    hbm = pl.BlockSpec(memory_space=pl.ANY)
    dma = pltpu.SemaphoreType.DMA
    halo = REACH * ttiles
    gains, changes = pl.pallas_call(
        functools.partial(kernel, dims),
        name="stefcal",
        out_shape=(
            jax.ShapeDtypeStruct(prior.shape, F32),
            jax.ShapeDtypeStruct((ITERS, width), F32),
        ),
        in_specs=[hbm, hbm, smem, smem, smem, vmem, vmem, vmem],
        out_specs=(vmem, vmem),
        scratch_shapes=[
            pltpu.VMEM((count,) + vis.shape[2:], BF16),
            pltpu.VMEM((count,) + vis.shape[2:], BF16),
            pltpu.VMEM((count * blks, 2 * width, 2 * width), BF16),
            pltpu.VMEM((count * blks, 2 * width, width), BF16),
            pltpu.VMEM((count, 2, nb, width), F32),
            pltpu.VMEM((count, 2, nb, width), F32),
            pltpu.VMEM((4, nb, width), F32),
            pltpu.VMEM(prior.shape[1:], F32),
            pltpu.VMEM((ITERS, count, 3, nb, width), F32),
            pltpu.VMEM((ITERS, halo, 3, nb, width), F32),
            pltpu.VMEM((ITERS, halo, 3, nb, width), F32),
            pltpu.VMEM((ITERS, ftiles, 3, nb, width), F32),
            pltpu.VMEM((ITERS, ftiles, 3, nb, width), F32),
            pltpu.VMEM((2 * ITERS, width), F32),
            pltpu.VMEM((nf, 2 * ITERS, width), F32),
            pltpu.VMEM((2 * ITERS, width), F32),
            pltpu.VMEM((nt, 2 * ITERS, width), F32),
            dma((2, count)),
            dma((2,)),
            dma((ITERS, halo)),
            dma((ITERS, halo)),
            dma((ITERS, halo)),
            dma((ITERS, halo)),
            dma((ITERS, ftiles)),
            dma((ITERS, ftiles)),
            dma((ITERS, ftiles)),
            dma((ITERS, ftiles)),
            dma((nf,)),
            dma((nf,)),
            dma((nt,)),
            dma((nt,)),
        ],
        compiler_params=pltpu.CompilerParams(
            collective_id=0, has_side_effects=True, vmem_limit_bytes=48 * 1024 * 1024
        ),
    )(vis, model, block_rows, block_cols, flags, prior, couplings, damping.reshape(1, -1))
    return gains, changes[:, 0]


def solution(mesh):
    placed = (
        P("freq", "tm", None, None, None, None),
        P("freq", "tm", None, None, None, None),
        P("freq", "tm", None),
        P("freq", "tm", None),
        P("freq", "tm", None),
        P("freq", "tm", None, None),
        P(),
        P(),
    )
    return jax.shard_map(
        per_device,
        mesh=mesh,
        in_specs=placed,
        out_specs=(P("freq", "tm", None, None), P()),
        check_vma=False,
    )
```

time: 136 us -> 52.3 us (0.38)
  Pallas kernels: 0 us -> 43.5 us
  blocking collectives: 41.1 us -> 0 us
  other arithmetic: 39.4 us -> 0 us
  starting transfers between devices: 38.9 us -> 0 us
  waiting for transfers between devices: 9.75 us -> 0 us
  local copies, waits for them, and re-layouts: 2.42 us -> 7.77 us
  matrix products: 2.56 us -> 0 us
    pallas_call x0 -> x1, Pallas kernels: none -> 43.5 us  [per_device(): pl.pallas_call(functools.partial(kernel, dims), name='stefcal', out_shape...]
    psum x1 -> x0, blocking collectives: 41.1 us -> none  [per_device(): change_all, scale_all = lax.psum((change_all, scale_all), ('freq', 'tm'))]
    ppermute x17 -> x0, starting transfers between devices: 38.9 us -> none  [the longest x8 24.1 us: extended(): lax.ppermute(lax.slice_in_dim(block, 0, width, axis=dim), axis, backward)]
    reduce_sum x5 -> x0, other arithmetic: 31.7 us -> none  [the longest x4 30.7 us: tile_terms(): num_re = jnp.sum(vis_re * zeta_re + vis_im * zeta_im, axis=-2)]
    ppermute x17 -> x0, waiting for transfers between devices: 9.75 us -> none  [the longest x8 8.78 us: extended(): lax.ppermute(lax.slice_in_dim(block, 0, width, axis=dim), axis, backward)]
    unnamed x13 -> x15, local copies, waits for them, and re-layouts: 0.77 us -> 7.15 us
    another operation x1 -> x0, other arithmetic: 5.01 us -> none  [per_device(): change_all = jnp.stack(change_list)]
    dot_general x8 -> x0, matrix products: 2.56 us -> none  [the longest x4 1.57 us: tile_terms(): jnp.einsum('kbn,kcnr->kbcr', row_hot, gain_blocks, precision=lax.Precisio...]
  transfers between devices with their start and end apart: 17 -> 0, of which waited for: 5 -> 0; matrix products, arithmetic and copies ran while one was open for 1% -> 0% of each run, Pallas kernels for 0% -> 0%
where the time goes in v1:
time: 52.3 us; the launch traced here: 51.9 us
  Pallas kernels  43.5 us (83%)
  local copies, waits for them, and re-layouts  7.77 us (15%)
  between operations  0.66 us (1%)
    pallas_call x1, Pallas kernels, per_device(): pl.pallas_call(functools.partial(kernel, dims), name='stefcal', out_shape...  43.5 us
    unnamed x15, local copies, waits for them, and re-layouts  7.15 us

profile of v1, /device:TPU:0, one launch (start us, length us, event | category | flops | bytes accessed | tf_op | source)
XLA Modules:
  0.0 51.9 jit_solution(10104605892167854889)
XLA Ops:
  0.6 0.0 copy-start
  0.6 2.2 %copy-done = bf16[2,2,16,2,128,128]{5,4,3,2,1,0:T(8,128)(2,1)S(1)} copy-done((bf16[2,2,16,2,128,128]{5,4,3,2,1,0:T(8,128)(2,1)S(1)}, bf16[2,2,16,2,128,128]{5,4,3,2,1,0:T(8,128)(2,1)}, u32[]{:S(2)}) %copy-start) | copy-done | bytes 4194328
  2.8 0.0 copy-start.1
  2.8 0.8 %copy-done.1 = f32[2,2,2,2048]{3,2,1,0:T(2,128)S(1)} copy-done((f32[2,2,2,2048]{3,2,1,0:T(2,128)S(1)}, f32[2,2,2,2048]{3,2,1,0:T(2,128)}, u32[]{:S(2)}) %copy-start.1) | copy-done | bytes 65560
  3.7 0.0 copy-start.2
  3.7 0.8 %copy-done.2 = f32[3,2048]{1,0:T(4,128)S(1)} copy-done((f32[3,2048]{1,0:T(4,128)S(1)}, f32[3,2048]{1,0:T(4,128)}, u32[]{:S(2)}) %copy-start.2) | copy-done | bytes 24600
  4.4 0.0 copy-start.3
  4.4 0.7 %copy-done.3 = f32[2048]{0:T(1024)S(1)} copy-done((f32[2048]{0:T(1024)S(1)}, f32[2048]{0:T(1024)}, u32[]{:S(2)}) %copy-start.3) | copy-done | bytes 8216
  5.1 0.0 copy-start.4
  5.1 0.7 %copy-done.4 = s32[2,2,16]{2,1,0:T(2,128)S(1)} copy-done((s32[2,2,16]{2,1,0:T(2,128)S(1)}, s32[2,2,16]{2,1,0:T(2,128)}, u32[]{:S(2)}) %copy-start.4) | copy-done | bytes 280
  5.8 0.0 copy-start.5
  5.8 0.7 %copy-done.5 = s32[2,2,16]{2,1,0:T(2,128)S(1)} copy-done((s32[2,2,16]{2,1,0:T(2,128)S(1)}, s32[2,2,16]{2,1,0:T(2,128)}, u32[]{:S(2)}) %copy-start.5) | copy-done | bytes 280
  6.5 0.0 copy-start.6
  6.5 0.7 %copy-done.6 = s32[2,2,16]{2,1,0:T(2,128)S(1)} copy-done((s32[2,2,16]{2,1,0:T(2,128)S(1)}, s32[2,2,16]{2,1,0:T(2,128)}, u32[]{:S(2)}) %copy-start.6) | copy-done | bytes 280
  7.2 43.5 %stefcal.1 = (f32[2,2,2,2048]{3,2,1,0:T(2,128)S(1)}, f32[4,128]{1,0:T(4,128)S(1)}) custom-call(bf16[2,2,16,2,128,128]{5,4,3,2,1,0:T(8,128)(2,1)S(1)} %copy-done, bf16[2,2,16,2,128,128]{5,4,3,2,1,0:T(8,128)(2,1)} %model_ref.1, s32[2,2,16]{2,1,0:T(2,128)S(1)} %copy-done.4, s32[2,2,16]{2,1,0:T(2,128)S(1)} %copy-done.5, s32[2,2,16]{2,1,0:T(2,128)S(1)} %copy-done.6, ...), custom_call_target="tpu_custom_call" | custom-call | tf_op jit(solution)/shard_map/stefcal/pallas_call | solution.py:328
  50.7 0.6 %slice_reduce_fusion = f32[4]{0:T(128)} fusion(f32[4,128]{1,0:T(4,128)S(1)} %get-tuple-element.5), kind=kLoop, calls=%fused_computation | loop fusion | bytes 32 | tf_op jit(solution)/shard_map/slice | solution.py:374
  51.3 0.6 %copy.11 = f32[2,2,2,2048]{3,2,1,0:T(2,128)} copy(f32[2,2,2,2048]{3,2,1,0:T(2,128)S(1)} %get-tuple-element.8) | data formatting | bytes 131072
Async XLA Ops:
  0.6 2.2 %copy-start = (bf16[2,2,16,2,128,128]{5,4,3,2,1,0:T(8,128)(2,1)S(1)}, bf16[2,2,16,2,128,128]{5,4,3,2,1,0:T(8,128)(2,1)}, u32[]{:S(2)}) copy-start(bf16[2,2,16,2,128,128]{5,4,3,2,1,0:T(8,128)(2,1)} %vis_ref.1) | copy-start | bytes 12582916
  2.8 0.8 %copy-start.1 = (f32[2,2,2,2048]{3,2,1,0:T(2,128)S(1)}, f32[2,2,2,2048]{3,2,1,0:T(2,128)}, u32[]{:S(2)}) copy-start(f32[2,2,2,2048]{3,2,1,0:T(2,128)} %prior_ref.1) | copy-start | bytes 196612
  3.7 0.8 %copy-start.2 = (f32[3,2048]{1,0:T(4,128)S(1)}, f32[3,2048]{1,0:T(4,128)}, u32[]{:S(2)}) copy-start(f32[3,2048]{1,0:T(4,128)} %coup_ref.1) | copy-start | bytes 73732
  4.4 0.7 %copy-start.3 = (f32[2048]{0:T(1024)S(1)}, f32[2048]{0:T(1024)}, u32[]{:S(2)}) copy-start(f32[2048]{0:T(1024)} %param.15) | copy-start | bytes 24580
  5.1 0.7 %copy-start.4 = (s32[2,2,16]{2,1,0:T(2,128)S(1)}, s32[2,2,16]{2,1,0:T(2,128)}, u32[]{:S(2)}) copy-start(s32[2,2,16]{2,1,0:T(2,128)} %rows_ref.1) | copy-start | bytes 772
  5.8 0.7 %copy-start.5 = (s32[2,2,16]{2,1,0:T(2,128)S(1)}, s32[2,2,16]{2,1,0:T(2,128)}, u32[]{:S(2)}) copy-start(s32[2,2,16]{2,1,0:T(2,128)} %cols_ref.1) | copy-start | bytes 772
  6.5 0.7 %copy-start.6 = (s32[2,2,16]{2,1,0:T(2,128)S(1)}, s32[2,2,16]{2,1,0:T(2,128)}, u32[]{:S(2)}) copy-start(s32[2,2,16]{2,1,0:T(2,128)} %flags_ref.1) | copy-start | bytes 772

commit v2 on v1

v2 whole, which is shorter than its diff:
```python
import functools

import jax
import jax.numpy as jnp
from jax import lax
from jax.experimental import pallas as pl
from jax.experimental.pallas import tpu as pltpu
from jax.sharding import PartitionSpec as P

ITERS = 4
REACH = 2
MESH = pl.DeviceIdType.MESH
F32 = jnp.float32
BF16 = jnp.bfloat16


def split(value):
    high = value.astype(BF16)
    return high, (value - high.astype(F32)).astype(BF16)


def kernel(
    dims,
    vis_ref, model_ref, rows_in, cols_in, flags_in, prior_in, coup_in, damp_in,
    gains_ref, changes_ref,
    rows_ref, cols_ref, flags_ref, prior_ref, coup_ref, damp_ref,
    vbuf, mbuf, wa, wb, gain, prev, coef, from_prior, terms, low, high, early, late,
    stats, all_stats,
    small_sem, load_sem, prior_sem, up_send, down_send, low_recv, high_recv,
    early_send, late_send, early_recv, late_recv, stats_send, stats_recv,
):
    nf, nt, ftiles, ttiles, blks, width, nb = dims
    fi = lax.axis_index("freq")
    ti = lax.axis_index("tm")
    above, below = lax.rem(fi + 1, nf), lax.rem(fi + nf - 1, nf)
    tiles = [(f, t) for f in range(ftiles) for t in range(ttiles)]

    devices = nf * nt
    me = fi * nt + ti

    def peer(step):
        other = lax.rem(me + step, devices)
        return other, {"freq": other // nt, "tm": lax.rem(other, nt)}

    small = [
        pltpu.make_async_copy(src, dst, small_sem.at[n])
        for n, (src, dst) in enumerate((
            (prior_in, prior_ref), (coup_in, coup_ref), (damp_in, damp_ref),
            (rows_in, rows_ref), (cols_in, cols_ref), (flags_in, flags_ref),
        ))
    ]
    for copy in small:
        copy.start()

    def loads(f, t):
        i = f * ttiles + t
        return (
            pltpu.make_async_copy(vis_ref.at[f, t], vbuf.at[i], load_sem.at[0, i]),
            pltpu.make_async_copy(model_ref.at[f, t], mbuf.at[i], load_sem.at[1, i]),
        )

    for f, t in tiles:
        for copy in loads(f, t):
            copy.start()

    barrier = pltpu.get_barrier_semaphore()

    def greet(step, carry):
        pl.semaphore_signal(barrier, inc=1, device_id=peer(step)[1], device_id_type=MESH)
        return carry

    lax.fori_loop(1, devices, greet, 0)
    for copy in small:
        copy.wait()

    for f, t in tiles:
        i = f * ttiles + t
        for c in range(2):
            for n in range(nb):
                gain[i, c, n : n + 1, :] = prior_ref[f, t, c : c + 1, n * width : (n + 1) * width]
    for n in range(nb):
        for c in range(3):
            coef[c, n : n + 1, :] = coup_ref[c : c + 1, n * width : (n + 1) * width]
        coef[3, n : n + 1, :] = damp_ref[0:1, n * width : (n + 1) * width]

    prior_copy = pltpu.make_async_remote_copy(
        src_ref=prior_ref.at[ftiles - 1], dst_ref=from_prior,
        send_sem=prior_sem.at[0], recv_sem=prior_sem.at[1],
        device_id={"freq": above}, device_id_type=MESH,
    )

    def up_copy(k, f, t):
        s = (f - (ftiles - REACH)) * ttiles + t
        return pltpu.make_async_remote_copy(
            src_ref=terms.at[k, f * ttiles + t], dst_ref=low.at[k, s],
            send_sem=up_send.at[k, s], recv_sem=low_recv.at[k, s],
            device_id={"freq": above}, device_id_type=MESH,
        )

    def down_copy(k, f, t):
        s = f * ttiles + t
        return pltpu.make_async_remote_copy(
            src_ref=terms.at[k, f * ttiles + t], dst_ref=high.at[k, s],
            send_sem=down_send.at[k, s], recv_sem=high_recv.at[k, s],
            device_id={"freq": below}, device_id_type=MESH,
        )

    def later_copy(k, f):
        return pltpu.make_async_remote_copy(
            src_ref=terms.at[k, f * ttiles + ttiles - 1], dst_ref=early.at[k, f],
            send_sem=early_send.at[k, f], recv_sem=early_recv.at[k, f],
            device_id={"tm": lax.rem(ti + 1, nt)}, device_id_type=MESH,
        )

    def earlier_copy(k, f):
        return pltpu.make_async_remote_copy(
            src_ref=terms.at[k, f * ttiles], dst_ref=late.at[k, f],
            send_sem=late_send.at[k, f], recv_sem=late_recv.at[k, f],
            device_id={"tm": lax.rem(ti + nt - 1, nt)}, device_id_type=MESH,
        )

    def prepare(i):
        def pair(p, carry):
            for side in range(2):
                b = 2 * p + side
                lo = side * width
                v_re = vbuf[i, b, 0].astype(F32)
                v_im = vbuf[i, b, 1].astype(F32)
                m_re = mbuf[i, b, 0].astype(F32)
                m_im = mbuf[i, b, 1].astype(F32)
                re_hi, re_lo = split(v_re * m_re + v_im * m_im)
                im_hi, im_lo = split(v_re * m_im - v_im * m_re)
                sq_hi, sq_lo = split(m_re * m_re + m_im * m_im)
                wa[i * blks + b, 0:width, 0:width] = re_hi
                wa[i * blks + b, width:, 0:width] = im_hi
                wa[i * blks + b, 0:width, width:] = sq_hi
                wa[i * blks + b, width:, width:] = sq_lo
                wb[i * (blks // 2) + p, 0:width, lo : lo + width] = re_lo
                wb[i * (blks // 2) + p, width:, lo : lo + width] = im_lo
            return carry

        lax.fori_loop(0, blks // 2, pair, 0)

    row_of = lax.broadcasted_iota(jnp.int32, (8, width), 0)
    block_of = lax.broadcasted_iota(jnp.int32, (nb, width), 0)

    def tile_terms(k, f, t):
        i = f * ttiles + t
        total = [jnp.zeros((nb, width), F32) for _ in range(3)]
        for p in range(blks // 2):
            highs, outs, cols = [], [], []
            for b in (2 * p, 2 * p + 1):
                row = rows_ref[f, t, b]
                cols.append(jnp.where(flags_ref[f, t, b] != 0, cols_ref[f, t, b], -1))
                re = jnp.broadcast_to(gain[i, 0, pl.ds(row, 1), :], (8, width))
                im = jnp.broadcast_to(gain[i, 1, pl.ds(row, 1), :], (8, width))
                sq = re * re + im * im
                left = jnp.where(row_of == 0, re, jnp.where(row_of == 1, im, sq))
                right = jnp.where(row_of == 0, -im, jnp.where(row_of == 1, re, sq))
                lhs = jnp.concatenate([left, right], axis=1)
                lhs_hi = lhs.astype(BF16).astype(F32)
                highs.append(lhs_hi)
                lhs = jnp.concatenate([lhs_hi, lhs - lhs_hi], axis=0).astype(BF16)
                out = jnp.dot(lhs, wa[i * blks + b], preferred_element_type=F32)
                outs.append(out[0:8] + out[8:16])
            low_out = jnp.dot(
                jnp.concatenate(highs, axis=0).astype(BF16),
                wb[i * (blks // 2) + p],
                preferred_element_type=F32,
            )
            low_outs = (low_out[0:8, 0:width], low_out[8:16, width:])
            for out, low_out, col in zip(outs, low_outs, cols):
                num = out[:, 0:width] + low_out
                den = out[:, width:]
                hit = block_of == col
                parts = (num[0:1], num[1:2], den[2:3])
                total = [
                    acc + jnp.where(hit, jnp.broadcast_to(one, (nb, width)), 0.0)
                    for acc, one in zip(total, parts)
                ]
        for c in range(3):
            terms[k, i, c] = total[c]

    def iteration(k, first):
        for f, t in tiles:
            i = f * ttiles + t
            if first:
                for copy in loads(f, t):
                    copy.wait()
                prepare(i)
            tile_terms(k, f, t)
            if first and i == 0:
                pl.semaphore_wait(barrier, devices - 1)
                prior_copy.start()
            if f >= ftiles - REACH:
                up_copy(k, f, t).start()
            if f < REACH:
                down_copy(k, f, t).start()
            if t == ttiles - 1:
                later_copy(k, f).start()
            if t == 0:
                earlier_copy(k, f).start()

        if first:
            prior_copy.wait_recv()
            for f, t in tiles:
                i = f * ttiles + t
                for c in range(2):
                    if f == 0:
                        for n in range(nb):
                            prev[i, c, n : n + 1, :] = from_prior[
                                t, c : c + 1, n * width : (n + 1) * width
                            ]
                        prev[i, c] = prev[i, c] * coef[3]
                    else:
                        prev[i, c] = gain[i - ttiles, c] * coef[3]

        for f in range(ftiles):
            later_copy(k, f).wait_recv()
            earlier_copy(k, f).wait_recv()
        for f in range(ftiles - REACH, ftiles):
            for t in range(ttiles):
                up_copy(k, f, t).wait_recv()
        for f in range(REACH):
            for t in range(ttiles):
                down_copy(k, f, t).wait_recv()

        def at(f, t, c):
            if t < 0:
                return jnp.where(ti > 0, early[k, f, c], 0.0)
            if t >= ttiles:
                return jnp.where(ti < nt - 1, late[k, f, c], 0.0)
            if f < 0:
                return low[k, (f + REACH) * ttiles + t, c]
            if f >= ftiles:
                return high[k, (f - ftiles) * ttiles + t, c]
            return terms[k, f * ttiles + t, c]

        odd = lax.rem(k, 2) == 1
        change = jnp.zeros((nb, width), F32)
        scale = jnp.zeros((nb, width), F32)
        for f, t in tiles:
            i = f * ttiles + t
            sums = [
                at(f, t, c)
                + coef[0] * (at(f - 1, t, c) + at(f + 1, t, c))
                + coef[1] * (at(f - 2, t, c) + at(f + 2, t, c))
                + coef[2] * (at(f, t - 1, c) + at(f, t + 1, c))
                for c in range(3)
            ]
            denom = sums[2] + coef[3]
            for c in range(2):
                old = gain[i, c]
                fresh = (sums[c] + prev[i, c]) / denom
                fresh = jnp.where(odd, 0.5 * (fresh + old), fresh)
                diff = fresh - old
                change = change + diff * diff
                scale = scale + fresh * fresh
                gain[i, c] = fresh
        sums = [
            jnp.sum(jnp.sum(x, axis=0, keepdims=True), axis=1, keepdims=True)
            for x in (change, scale)
        ]
        stats[...] = jnp.where(lane_of == k, jnp.concatenate(sums, axis=0), stats[...])

    lane_of = lax.broadcasted_iota(jnp.int32, (2, width), 1)
    stats[...] = jnp.zeros_like(stats)
    iteration(0, True)

    def rest(k, carry):
        iteration(k, False)
        return carry

    lax.fori_loop(1, ITERS, rest, 0)

    def stats_copy(step, slot):
        return pltpu.make_async_remote_copy(
            src_ref=stats, dst_ref=all_stats.at[slot],
            send_sem=stats_send.at[step], recv_sem=stats_recv.at[slot],
            device_id=peer(step)[1], device_id_type=MESH,
        )

    def send_stats(step, carry):
        stats_copy(step, me).start()
        return carry

    lax.fori_loop(1, devices, send_stats, 0)
    all_stats[me] = stats[...]

    for f, t in tiles:
        i = f * ttiles + t
        for c in range(2):
            for n in range(nb):
                gains_ref[f, t, c : c + 1, n * width : (n + 1) * width] = gain[i, c, n : n + 1, :]

    def drain(k, carry):
        for f, t in tiles:
            if f >= ftiles - REACH:
                up_copy(k, f, t).wait_send()
            if f < REACH:
                down_copy(k, f, t).wait_send()
        for f in range(ftiles):
            later_copy(k, f).wait_send()
            earlier_copy(k, f).wait_send()
        return carry

    lax.fori_loop(0, ITERS, drain, 0)
    prior_copy.wait_send()

    def finish(step, carry):
        stats_copy(step, me).wait_send()
        stats_copy(step, peer(step)[0]).wait_recv()
        return carry

    lax.fori_loop(1, devices, finish, 0)
    whole = jnp.sum(all_stats[...], axis=0)
    changes_ref[...] = jnp.sqrt(whole[0:1] / (whole[1:2] + 1e-06))


def per_device(vis, model, block_rows, block_cols, flags, prior, couplings, damping):
    nf, nt = lax.axis_size("freq"), lax.axis_size("tm")
    ftiles, ttiles, blks = vis.shape[:3]
    width = vis.shape[-1]
    nb = prior.shape[-1] // width
    count = ftiles * ttiles
    dims = (nf, nt, ftiles, ttiles, blks, width, nb)
    vmem = pl.BlockSpec(memory_space=pltpu.VMEM)
    hbm = pl.BlockSpec(memory_space=pltpu.HBM)
    dma = pltpu.SemaphoreType.DMA
    halo = REACH * ttiles
    gains, changes = pl.pallas_call(
        functools.partial(kernel, dims),
        name="stefcal",
        out_shape=(
            jax.ShapeDtypeStruct(prior.shape, F32),
            jax.ShapeDtypeStruct((1, width), F32),
        ),
        in_specs=[hbm] * 8,
        out_specs=(vmem, vmem),
        scratch_shapes=[
            pltpu.SMEM(block_rows.shape, jnp.int32),
            pltpu.SMEM(block_rows.shape, jnp.int32),
            pltpu.SMEM(block_rows.shape, jnp.int32),
            pltpu.VMEM(prior.shape, F32),
            pltpu.VMEM(couplings.shape, F32),
            pltpu.VMEM((1, damping.shape[0]), F32),
            pltpu.VMEM((count,) + vis.shape[2:], BF16),
            pltpu.VMEM((count,) + vis.shape[2:], BF16),
            pltpu.VMEM((count * blks, 2 * width, 2 * width), BF16),
            pltpu.VMEM((count * blks // 2, 2 * width, 2 * width), BF16),
            pltpu.VMEM((count, 2, nb, width), F32),
            pltpu.VMEM((count, 2, nb, width), F32),
            pltpu.VMEM((4, nb, width), F32),
            pltpu.VMEM(prior.shape[1:], F32),
            pltpu.VMEM((ITERS, count, 3, nb, width), F32),
            pltpu.VMEM((ITERS, halo, 3, nb, width), F32),
            pltpu.VMEM((ITERS, halo, 3, nb, width), F32),
            pltpu.VMEM((ITERS, ftiles, 3, nb, width), F32),
            pltpu.VMEM((ITERS, ftiles, 3, nb, width), F32),
            pltpu.VMEM((2, width), F32),
            pltpu.VMEM((nf * nt, 2, width), F32),
            dma((6,)),
            dma((2, count)),
            dma((2,)),
            dma((ITERS, halo)),
            dma((ITERS, halo)),
            dma((ITERS, halo)),
            dma((ITERS, halo)),
            dma((ITERS, ftiles)),
            dma((ITERS, ftiles)),
            dma((ITERS, ftiles)),
            dma((ITERS, ftiles)),
            dma((nf * nt,)),
            dma((nf * nt,)),
        ],
        compiler_params=pltpu.CompilerParams(
            collective_id=0, has_side_effects=True, vmem_limit_bytes=48 * 1024 * 1024
        ),
    )(vis, model, block_rows, block_cols, flags, prior, couplings, damping.reshape(1, -1))
    return gains, changes[0, :ITERS]


def solution(mesh):
    placed = (
        P("freq", "tm", None, None, None, None),
        P("freq", "tm", None, None, None, None),
        P("freq", "tm", None),
        P("freq", "tm", None),
        P("freq", "tm", None),
        P("freq", "tm", None, None),
        P(),
        P(),
    )
    return jax.shard_map(
        per_device,
        mesh=mesh,
        in_specs=placed,
        out_specs=(P("freq", "tm", None, None), P()),
        check_vma=False,
    )
```

time: 52.3 us -> 50.1 us (0.958)
  Pallas kernels: 43.5 us -> 41.4 us
    pallas_call x1, Pallas kernels: 43.5 us -> 41.4 us  [per_device(): pl.pallas_call(functools.partial(kernel, dims), name='stefcal', out_shape...]
    slice x1 -> x0, local copies, waits for them, and re-layouts: 0.63 us -> none  [per_device(): return (gains, changes[:, 0])]
where the time goes in v2:
time: 50.1 us; the launch traced here: 49.7 us
  Pallas kernels  41.4 us (83%)
  local copies, waits for them, and re-layouts  7.66 us (15%)
  between operations  0.66 us (1%)
    pallas_call x1, Pallas kernels, per_device(): pl.pallas_call(functools.partial(kernel, dims), name='stefcal', out_shape...  41.4 us
    unnamed x15, local copies, waits for them, and re-layouts  7.15 us

profile of v2, /device:TPU:0, one launch (start us, length us, event | category | flops | bytes accessed | tf_op | source)
XLA Modules:
  0.0 49.7 jit_solution(6324966653253870997)
XLA Ops:
  0.6 0.0 copy-start
  0.6 2.2 %copy-done = bf16[2,2,16,2,128,128]{5,4,3,2,1,0:T(8,128)(2,1)S(1)} copy-done((bf16[2,2,16,2,128,128]{5,4,3,2,1,0:T(8,128)(2,1)S(1)}, bf16[2,2,16,2,128,128]{5,4,3,2,1,0:T(8,128)(2,1)}, u32[]{:S(2)}) %copy-start) | copy-done | bytes 4194328
  2.8 0.0 copy-start.1
  2.8 0.8 %copy-done.1 = f32[2,2,2,2048]{3,2,1,0:T(2,128)S(1)} copy-done((f32[2,2,2,2048]{3,2,1,0:T(2,128)S(1)}, f32[2,2,2,2048]{3,2,1,0:T(2,128)}, u32[]{:S(2)}) %copy-start.1) | copy-done | bytes 65560
  3.7 0.0 copy-start.2
  3.7 0.8 %copy-done.2 = f32[3,2048]{1,0:T(4,128)S(1)} copy-done((f32[3,2048]{1,0:T(4,128)S(1)}, f32[3,2048]{1,0:T(4,128)}, u32[]{:S(2)}) %copy-start.2) | copy-done | bytes 24600
  4.4 0.0 copy-start.3
  4.4 0.7 %copy-done.3 = f32[2048]{0:T(1024)S(1)} copy-done((f32[2048]{0:T(1024)S(1)}, f32[2048]{0:T(1024)}, u32[]{:S(2)}) %copy-start.3) | copy-done | bytes 8216
  5.1 0.0 copy-start.4
  5.1 0.7 %copy-done.4 = s32[2,2,16]{2,1,0:T(2,128)S(1)} copy-done((s32[2,2,16]{2,1,0:T(2,128)S(1)}, s32[2,2,16]{2,1,0:T(2,128)}, u32[]{:S(2)}) %copy-start.4) | copy-done | bytes 280
  5.8 0.0 copy-start.5
  5.8 0.7 %copy-done.5 = s32[2,2,16]{2,1,0:T(2,128)S(1)} copy-done((s32[2,2,16]{2,1,0:T(2,128)S(1)}, s32[2,2,16]{2,1,0:T(2,128)}, u32[]{:S(2)}) %copy-start.5) | copy-done | bytes 280
  6.5 0.0 copy-start.6
  6.5 0.7 %copy-done.6 = s32[2,2,16]{2,1,0:T(2,128)S(1)} copy-done((s32[2,2,16]{2,1,0:T(2,128)S(1)}, s32[2,2,16]{2,1,0:T(2,128)}, u32[]{:S(2)}) %copy-start.6) | copy-done | bytes 280
  7.2 41.4 %stefcal.1 = (f32[2,2,2,2048]{3,2,1,0:T(2,128)S(1)}, f32[1,128]{1,0:T(1,128)S(1)}) custom-call(bf16[2,2,16,2,128,128]{5,4,3,2,1,0:T(8,128)(2,1)S(1)} %copy-done, bf16[2,2,16,2,128,128]{5,4,3,2,1,0:T(8,128)(2,1)} %model_ref.1, s32[2,2,16]{2,1,0:T(2,128)S(1)} %copy-done.4, s32[2,2,16]{2,1,0:T(2,128)S(1)} %copy-done.5, s32[2,2,16]{2,1,0:T(2,128)S(1)} %copy-done.6, ...), custom_call_target="tpu_custom_call" | custom-call | tf_op jit(solution)/shard_map/stefcal/pallas_call | solution.py:331
  48.6 0.5 %slice_bitcast_fusion = f32[4]{0:T(128)} fusion(f32[1,128]{1,0:T(1,128)S(1)} %get-tuple-element.5), kind=kLoop, calls=%fused_computation | loop fusion | bytes 32 | tf_op jit(solution)/shard_map/squeeze | solution.py:380
  49.1 0.6 %copy.11 = f32[2,2,2,2048]{3,2,1,0:T(2,128)} copy(f32[2,2,2,2048]{3,2,1,0:T(2,128)S(1)} %get-tuple-element.8) | data formatting | bytes 131072
Async XLA Ops:
  0.6 2.2 %copy-start = (bf16[2,2,16,2,128,128]{5,4,3,2,1,0:T(8,128)(2,1)S(1)}, bf16[2,2,16,2,128,128]{5,4,3,2,1,0:T(8,128)(2,1)}, u32[]{:S(2)}) copy-start(bf16[2,2,16,2,128,128]{5,4,3,2,1,0:T(8,128)(2,1)} %vis_ref.1) | copy-start | bytes 12582916
  2.8 0.8 %copy-start.1 = (f32[2,2,2,2048]{3,2,1,0:T(2,128)S(1)}, f32[2,2,2,2048]{3,2,1,0:T(2,128)}, u32[]{:S(2)}) copy-start(f32[2,2,2,2048]{3,2,1,0:T(2,128)} %prior_in.1) | copy-start | bytes 196612
  3.7 0.8 %copy-start.2 = (f32[3,2048]{1,0:T(4,128)S(1)}, f32[3,2048]{1,0:T(4,128)}, u32[]{:S(2)}) copy-start(f32[3,2048]{1,0:T(4,128)} %coup_in.1) | copy-start | bytes 73732
  4.4 0.7 %copy-start.3 = (f32[2048]{0:T(1024)S(1)}, f32[2048]{0:T(1024)}, u32[]{:S(2)}) copy-start(f32[2048]{0:T(1024)} %param.15) | copy-start | bytes 24580
  5.1 0.7 %copy-start.4 = (s32[2,2,16]{2,1,0:T(2,128)S(1)}, s32[2,2,16]{2,1,0:T(2,128)}, u32[]{:S(2)}) copy-start(s32[2,2,16]{2,1,0:T(2,128)} %rows_in.1) | copy-start | bytes 772
  5.8 0.7 %copy-start.5 = (s32[2,2,16]{2,1,0:T(2,128)S(1)}, s32[2,2,16]{2,1,0:T(2,128)}, u32[]{:S(2)}) copy-start(s32[2,2,16]{2,1,0:T(2,128)} %cols_in.1) | copy-start | bytes 772
  6.5 0.7 %copy-start.6 = (s32[2,2,16]{2,1,0:T(2,128)S(1)}, s32[2,2,16]{2,1,0:T(2,128)}, u32[]{:S(2)}) copy-start(s32[2,2,16]{2,1,0:T(2,128)} %flags_in.1) | copy-start | bytes 772

commit v3 on v2

--- a/solution.py
+++ b/solution.py
@@ -374,7 +374,7 @@
             dma((nf * nt,)),
         ],
         compiler_params=pltpu.CompilerParams(
-            collective_id=0, has_side_effects=True, vmem_limit_bytes=48 * 1024 * 1024
+            collective_id=0, has_side_effects=True, vmem_limit_bytes=67043328
         ),
     )(vis, model, block_rows, block_cols, flags, prior, couplings, damping.reshape(1, -1))
     return gains, changes[0, :ITERS]

time: 50.1 us -> 46.3 us (0.924)
  local copies, waits for them, and re-layouts: 7.66 us -> 2.59 us
  Pallas kernels: 41.4 us -> 42.9 us
    unnamed x15 -> x1, local copies, waits for them, and re-layouts: 7.15 us -> 1.47 us
    pallas_call x1, Pallas kernels: 41.4 us -> 42.9 us  [per_device(): pl.pallas_call(functools.partial(kernel, dims), name='stefcal', out_shape...]
    squeeze x1, local copies, waits for them, and re-layouts: 0.51 us -> 1.12 us  [per_device(): return (gains, changes[0, :ITERS])]
where the time goes in v3:
time: 46.3 us; the launch traced here: 46.1 us
  Pallas kernels  42.9 us (93%)
  local copies, waits for them, and re-layouts  2.59 us (6%)
  between operations  0.64 us (1%)
    pallas_call x1, Pallas kernels, per_device(): pl.pallas_call(functools.partial(kernel, dims), name='stefcal', out_shape...  42.9 us
    unnamed x1, local copies, waits for them, and re-layouts  1.47 us
    squeeze x1, local copies, waits for them, and re-layouts, per_device(): return (gains, changes[0, :ITERS])  1.12 us

profile of v3, /device:TPU:0, one launch (start us, length us, event | category | flops | bytes accessed | tf_op | source)
XLA Modules:
  0.0 46.1 jit_solution(10804100489541264634)
XLA Ops:
  0.6 42.9 %stefcal.1 = (f32[2,2,2,2048]{3,2,1,0:T(2,128)}, f32[1,128]{1,0:T(1,128)}) custom-call(bf16[2,2,16,2,128,128]{5,4,3,2,1,0:T(8,128)(2,1)} %vis_ref.1, bf16[2,2,16,2,128,128]{5,4,3,2,1,0:T(8,128)(2,1)} %model_ref.1, s32[2,2,16]{2,1,0:T(2,128)} %rows_in.1, s32[2,2,16]{2,1,0:T(2,128)} %cols_in.1, s32[2,2,16]{2,1,0:T(2,128)} %flags_in.1, ...), custom_call_target="tpu_custom_call" | custom-call | tf_op jit(solution)/shard_map/stefcal/pallas_call | solution.py:331
  43.5 1.1 %slice_bitcast_fusion = f32[4]{0:T(128)} fusion(f32[1,128]{1,0:T(1,128)} %get-tuple-element.5), kind=kLoop, calls=%fused_computation | loop fusion | bytes 32 | tf_op jit(solution)/shard_map/squeeze | solution.py:380
  44.7 1.5 %copy.11 = f32[2,2,2,2048]{3,2,1,0:T(2,128)} copy(f32[2,2,2,2048]{3,2,1,0:T(2,128)} %get-tuple-element.8) | data formatting | bytes 131072
